TPU v7x, 512 devices: a whole 4x4x16 slice. The times are simulated.
512 devices in a mesh: ctx: 64 (over z, y), tp: 8 (over x, core).
Axes of the slice: x: 4, y: 4, z: 16, core: 2. Of those that a mesh axis runs over, the one named last changes fastest.
Arguments:
- rotated_asking_vectors: bfloat16 [2, 2048, 64, 128], P(None, ('ctx', 'tp')), may hold values from -6 to 6
- rotated_match_vectors: bfloat16 [2, 2048, 8, 128], P(None, ('ctx', 'tp')), may hold values from -6 to 6
- content_vectors: bfloat16 [2, 2048, 8, 128], P(None, ('ctx', 'tp')), may hold values from -6 to 6
- result_cotangent: bfloat16 [2, 2048, 64, 128], P(None, ('ctx', 'tp')), may hold values from -6 to 6
Outputs:
- attended: bfloat16 [2, 2048, 64, 128], P(None, ('ctx', 'tp'))
- grad_query: bfloat16 [2, 2048, 64, 128], P(None, ('ctx', 'tp'))
- grad_key: bfloat16 [2, 2048, 8, 128], P(None, ('ctx', 'tp'))
- grad_value: bfloat16 [2, 2048, 8, 128], P(None, ('ctx', 'tp'))
All inputs are finite; a program needn't handle non-finite values.
Results may differ from a plain program's by a relative error of at most 0.002.
Values may be sent and summed in bfloat16 or wider, within the bound.
A program may use at most 64 MiB of HBM per device.

v0:
```python
from functools import partial

import jax
import jax.numpy as jnp
from jax import lax
from jax.experimental import pallas as pl
from jax.experimental.pallas import tpu as pltpu
from jax.sharding import PartitionSpec as P

MESH = pl.DeviceIdType.MESH
masked_score = -1e30
F32, BF16 = jnp.float32, jnp.bfloat16


def dot(a, b, dims=((1,), (0,))):
    return lax.dot_general(a, b, (dims, ((), ())), preferred_element_type=F32)


def halves(x):
    high = x.astype(BF16)
    return high, (x - high.astype(F32)).astype(BF16)


def kernel(
    sizes,
    q_ref,
    g_ref,
    kv_ref,
    att_ref,
    dq_ref,
    okv_ref,
    qgb,
    kvb,
    out_qg,
    acc,
    recv,
    out_kv,
    wide,
    turned,
    kv_s,
    kv_r,
    qg_s,
    qg_r,
    z_s,
    z_r,
    p_s,
    p_r,
    o_s,
    o_r,
    f_s,
    f_r,
    local,
):
    layers, inner, outer, tp_n, t, heads, width = sizes
    G = inner * tp_n
    B = G * t
    T = outer * B
    rows = t * heads
    scale = width**-0.5
    ctx, tp = lax.axis_index("ctx"), lax.axis_index("tp")
    z = ctx // inner
    me = (ctx % inner) * tp_n + tp

    def in_plane(peer):
        return {"ctx": z * inner + peer // tp_n, "tp": peer % tp_n}

    def in_column(o):
        return {"ctx": o * inner + ctx % inner, "tp": tp}

    def kv_copy(l, to, slot):
        return pltpu.make_async_remote_copy(
            kv_ref.at[to, l], kvb.at[l, z, slot], kv_s.at[l, to], kv_r.at[l, slot], in_plane(to), MESH
        )

    def group(ref, l, peer):
        return ref.at[l, :, pl.ds(pl.multiple_of(peer * heads, heads), heads), :]

    def qg_copy(l, kind, to, slot):
        return pltpu.make_async_remote_copy(
            group((q_ref, g_ref)[kind], l, to),
            qgb.at[l, slot, kind],
            qg_s.at[l, kind, to],
            qg_r.at[l, kind, slot],
            in_plane(to),
            MESH,
        )

    def z_copy(l, to, slot):
        return pltpu.make_async_remote_copy(
            kvb.at[l, slot], kvb.at[l, slot], z_s.at[l, to], z_r.at[l, slot], in_column(to), MESH
        )

    def p_copy(l, to, slot):
        return pltpu.make_async_remote_copy(
            acc.at[l, to], recv.at[l, slot], p_s.at[l, to], p_r.at[l, slot], in_column(to), MESH
        )

    def o_copy(l, kind, to, slot):
        return pltpu.make_async_remote_copy(
            out_qg.at[l, to, kind],
            group((att_ref, dq_ref)[kind], l, slot),
            o_s.at[l, kind, to],
            o_r.at[l, kind, slot],
            in_plane(to),
            MESH,
        )

    def o_own(l, kind):
        return pltpu.make_async_copy(
            out_qg.at[l, me, kind], group((att_ref, dq_ref)[kind], l, me), local.at[l, 3 + kind]
        )

    def f_copy(l, to, slot):
        return pltpu.make_async_remote_copy(
            out_kv.at[l, to], okv_ref.at[slot, l], f_s.at[l, to], f_r.at[l, slot], in_plane(to), MESH
        )

    def each_peer(fn):
        for d in range(1, G):
            fn(lax.rem(me + d, G))

    barrier = pltpu.get_barrier_semaphore()
    each_peer(lambda p: pl.semaphore_signal(barrier, 1, device_id=in_plane(p), device_id_type=MESH))

    @pl.loop(1, outer)
    def _(d):
        pl.semaphore_signal(
            barrier, 1, device_id=in_column(lax.rem(z + d, outer)), device_id_type=MESH
        )

    pl.semaphore_wait(barrier, G - 1 + outer - 1)

    for l in range(layers):
        each_peer(lambda p: kv_copy(l, p, me).start())
    for l in range(layers):
        for kind in range(2):
            each_peer(lambda p: qg_copy(l, kind, p, me).start())
    own = []
    for l in range(layers):
        own.append(pltpu.make_async_copy(kv_ref.at[me, l], kvb.at[l, z, me], local.at[l, 0]))
        for kind, ref in enumerate((q_ref, g_ref)):
            own.append(
                pltpu.make_async_copy(group(ref, l, me), qgb.at[l, me, kind], local.at[l, 1 + kind])
            )
    for copy in own:
        copy.start()
    for l in range(layers):

        @pl.loop(z + 1, outer)
        def _(o):
            kvb[l, o] = jnp.zeros(kvb.shape[2:], BF16)

    for copy in own:
        copy.wait()
    for l in range(layers):
        each_peer(lambda p: kv_copy(l, me, p).wait_recv())

        @pl.loop(z + 1, outer)
        def _(o):
            z_copy(l, o, z).start()

    n = max(1, min(G, 256 // rows))
    c = n * rows

    def whole(l, kind):
        if t % 16 == 0:
            return kvb[l, :, :, kind].reshape(T, width)
        return wide[kind].reshape(T, width).astype(BF16)

    for l in range(layers):
        for kind in range(2):
            each_peer(lambda p: qg_copy(l, kind, me, p).wait_recv())

        @pl.loop(0, z)
        def _(o):
            z_copy(l, me * 0 + o, o).wait_recv()

        if t % 16:

            @pl.loop(0, outer)
            def _(o):
                for p in range(G):
                    for kind in range(2):
                        wide[kind, o, p * t : (p + 1) * t, :] = kvb[l, o, p, kind].astype(F32)

        for kind in range(2):
            turned[kind] = whole(l, kind).astype(F32).T.astype(BF16)
        acc[l] = jnp.zeros(acc.shape[1:], F32)

        @pl.loop(0, G // n)
        def _(ci):
            K, V = whole(l, 0), whole(l, 1)
            span = pl.ds(ci * n, n)
            Q = qgb[l, span, 0].reshape(c, width)
            dO = qgb[l, span, 1].reshape(c, width)
            token = z * B + (ci * c + lax.broadcasted_iota(jnp.int32, (1, c), 1)) // heads
            allowed = lax.broadcasted_iota(jnp.int32, (T, c), 0) <= token
            scores = jnp.where(allowed, dot(K, Q, ((1,), (1,))) * scale, masked_score)
            e = jnp.exp(scores - jnp.max(scores, axis=0, keepdims=True))
            prob = e * (1.0 / jnp.sum(e, axis=0, keepdims=True))
            ph, pe = halves(prob)
            att = (dot(turned[1], ph) + dot(turned[1], pe)).T.astype(BF16)
            out_qg[l, span, 0] = att.reshape(n, t, heads, width)
            delta = jnp.sum((att.astype(F32) * dO.astype(F32)).T, axis=0, keepdims=True)
            dscore = prob * (dot(V, dO, ((1,), (1,))) - delta)
            dh, de = halves(dscore)
            dq = ((dot(turned[0], dh) + dot(turned[0], de)) * scale).T.astype(BF16)
            out_qg[l, span, 1] = dq.reshape(n, t, heads, width)
            acc[l, :, 0] += (dot(dh, Q) + dot(de, Q)).reshape(outer, B, width)
            acc[l, :, 1] += (dot(ph, dO) + dot(pe, dO)).reshape(outer, B, width)
            for i in range(n):
                peer = ci * n + i

                @pl.when(peer != me)
                def _():
                    for kind in range(2):
                        o_copy(l, kind, peer, me).start()

        @pl.loop(0, z)
        def _(o):
            p_copy(l, o, z).start()

        for kind in range(2):
            o_own(l, kind).start()

    for l in range(layers):

        @pl.loop(z + 1, outer)
        def _(o):
            p_copy(l, z, o).wait_recv()
            acc[l, z] += recv[l, o]

        for kind in range(2):
            factor = scale if kind == 0 else 1.0
            for p in range(G):
                out_kv[l, p, kind] = (acc[l, z, kind, p * t : (p + 1) * t, :] * factor).astype(BF16)
        each_peer(lambda p: f_copy(l, p, me).start())
        pltpu.make_async_copy(out_kv.at[l, me], okv_ref.at[me, l], local.at[l, 5]).start()

    for l in range(layers):
        for kind in range(2):
            o_own(l, kind).wait()
        pltpu.make_async_copy(out_kv.at[l, me], okv_ref.at[me, l], local.at[l, 5]).wait()

        def finish(p):
            kv_copy(l, p, me).wait_send()
            for kind in range(2):
                qg_copy(l, kind, p, me).wait_send()
                o_copy(l, kind, p, me).wait_send()
                o_copy(l, kind, me, p).wait_recv()
            f_copy(l, p, me).wait_send()
            f_copy(l, me, p).wait_recv()

        each_peer(finish)

        @pl.loop(z + 1, outer)
        def _(o):
            z_copy(l, o, z).wait_send()

        @pl.loop(0, z)
        def _(o):
            p_copy(l, o, z).wait_send()


def on_device(q, k, v, g):
    layers, t, head_count, width = q.shape
    kv_heads = k.shape[2]
    heads = head_count // kv_heads
    ctx_n, tp_n = lax.axis_size("ctx"), lax.axis_size("tp")
    inner = kv_heads // tp_n
    outer = ctx_n // inner
    G, B = kv_heads, kv_heads * t

    def pack(a, b):
        both = jnp.stack([a, b]).reshape(2, layers, t, kv_heads, -1, width)
        return both.transpose(3, 1, 0, 2, 4, 5).reshape(kv_heads, layers, 2, -1, width)

    def unpack(both):
        both = both.reshape(kv_heads, layers, 2, t, -1, width).transpose(2, 1, 3, 0, 4, 5)
        both = both.reshape(2, layers, t, -1, width)
        return both[0], both[1]

    vmem = pl.BlockSpec(memory_space=pltpu.VMEM)
    sem = pltpu.SemaphoreType.DMA
    plane, column = sem((layers, G)), sem((layers, outer))
    pair = sem((layers, 2, G))
    whole_shape = jax.ShapeDtypeStruct(q.shape, BF16)
    kv_shape = (kv_heads, layers, 2, t, width)
    attended, grad_query, okv = pl.pallas_call(
        partial(kernel, (layers, inner, outer, tp_n, t, heads, width)),
        out_shape=(whole_shape, whole_shape, jax.ShapeDtypeStruct(kv_shape, BF16)),
        in_specs=[vmem, vmem, vmem],
        out_specs=(vmem, vmem, vmem),
        scratch_shapes=[
            pltpu.VMEM((layers, G, 2, t, heads, width), BF16),
            pltpu.VMEM((layers, outer, G, 2, t, width), BF16),
            pltpu.VMEM((layers, G, 2, t, heads, width), BF16),
            pltpu.VMEM((layers, outer, 2, B, width), F32),
            pltpu.VMEM((layers, outer, 2, B, width), F32),
            pltpu.VMEM((layers, G, 2, t, width), BF16),
            pltpu.VMEM((2, outer, B, width) if t % 16 else (2, 1, 8, width), F32),
            pltpu.VMEM((2, width, outer * B), BF16),
            plane,
            plane,
            pair,
            pair,
            column,
            column,
            column,
            column,
            pair,
            pair,
            plane,
            plane,
            sem((layers, 6)),
        ],
        compiler_params=pltpu.CompilerParams(collective_id=0, has_side_effects=True),
    )(q, g, pack(k, v))
    grad_key, grad_value = unpack(okv)
    return attended, grad_query, grad_key, grad_value


def solution(mesh):
    spec = P(None, ("ctx", "tp"), None, None)
    return jax.shard_map(
        on_device, mesh=mesh, in_specs=(spec,) * 4, out_specs=(spec,) * 4, check_vma=False
    )
```

profile of v0, /device:TPU:193, one launch (start us, length us, event | category | flops | bytes accessed | tf_op | source)
XLA Modules:
  0.0 312.1 jit_solution(3040954003375754926)
XLA Ops:
  0.6 0.7 copy_bitcast_fusion
  1.4 0.6 maximum_bitcast_fusion.kv_ref
  2.0 306.5 %shard_map.75 = (bf16[2,4,64,128]{3,2,1,0:T(8,128)(2,1)}, bf16[2,4,64,128]{3,2,1,0:T(8,128)(2,1)}, bf16[8,2,2,4,128]{4,3,2,1,0:T(4,128)(2,1)}) custom-call(bf16[2,4,64,128]{3,2,1,0:T(8,128)(2,1)} %q_ref.1, bf16[2,4,64,128]{3,2,1,0:T(8,128)(2,1)} %g_ref.1, bf16[8,2,2,4,128]{4,3,2,1,0:T(4,128)(2,1)} %maximum_bitcast_fusion.kv_ref), custom_call_target="tpu_custom_call" | custom-call | tf_op jit(solution)/shard_map/pallas_call | solution.py:289
  308.5 0.0 copy-start.1
  308.5 0.8 slice_bitcast_fusion
  309.3 0.6 copy.11
  309.9 0.6 copy.10
  310.5 0.0 copy-done.1
  310.5 0.0 copy-start
  310.5 0.7 copy.16
  311.2 0.3 copy-done
  311.5 0.7 copy.17
Async XLA Ops:
  308.5 2.0 copy-start.1
  310.5 1.0 copy-start
where the time goes:
time: 312 us
  Pallas kernels  306 us (98%)
  local copies, waits for them, and re-layouts  4.36 us (1%)
    pallas_call x1, Pallas kernels, on_device(): pl.pallas_call(partial(kernel, (layers, inner, outer, tp_n, t, heads, wid...  306 us

commit v1 on v0

v1 whole, which is shorter than its diff:
```python
from functools import partial

import jax
import jax.numpy as jnp
from jax import lax
from jax.experimental import pallas as pl
from jax.experimental.pallas import tpu as pltpu
from jax.sharding import PartitionSpec as P

MESH = pl.DeviceIdType.MESH
F32, BF16 = jnp.float32, jnp.bfloat16
masked_score = -1e30
NX, CORES = 4, 2
REACH = 1


def dot(a, b):
    return lax.dot_general(a, b, (((1,), (0,)), ((), ())), preferred_element_type=F32)


def kernel(
    sizes,
    q_ref,
    k_ref,
    v_ref,
    g_ref,
    att_ref,
    dq_ref,
    gk_ref,
    gv_ref,
    narrow,
    kvp,
    kvin,
    qin,
    kv,
    qs,
    gs,
    qt,
    gt,
    top,
    sc,
    dp,
    pb,
    db,
    kt2,
    vt2,
    att_t,
    dq_t,
    acc,
    pin,
    recv,
    oq,
    okv,
    okv_in,
    kv_s,
    kv_r,
    q_s,
    q_r,
    g_s,
    g_r,
    h_s,
    h_r,
    p_s,
    p_r,
    r_s,
    r_r,
    o_s,
    o_r,
    f_s,
    f_r,
    local,
):
    layers, G, nx, ny, NZ, t, heads, width = sizes
    PN = nx * ny
    H = NZ // 2
    R = REACH
    HK = PN * t
    BK = 2 * HK
    rows = PN * t * heads
    scale = width**-0.5
    ctx, tp = lax.axis_index("ctx"), lax.axis_index("tp")
    z, y = ctx // ny, ctx % ny
    x, c = tp // CORES, tp % CORES
    me = y * nx + x

    def at(p, core):
        return {"ctx": z * ny + p // nx, "tp": (p % nx) * CORES + core}

    def up(i):
        return {"ctx": lax.rem(z + i, NZ) * ny + y, "tp": tp}

    def down(i):
        return {"ctx": lax.rem(z + NZ - i, NZ) * ny + y, "tp": tp}

    partner = {"ctx": ctx, "tp": x * CORES + 1 - c}

    def remote(src, dst, s, r, to):
        return pltpu.make_async_remote_copy(src, dst, s, r, to, MESH)

    def group(ref, p):
        return ref.at[p // G, :, pl.ds(pl.multiple_of((p % G) * heads, heads), heads), :]

    def kv_copy(to, core, src_core, src):
        return remote(kvp.at[to], kvin.at[src_core, src], kv_s.at[core, to], kv_r.at[src_core, src], at(to, core))

    def q_copy(kind, to, src):
        return remote(
            group((q_ref, g_ref)[kind], to), qin.at[kind, src], q_s.at[kind, to], q_r.at[kind, src], at(to, c)
        )

    def g_copy(plus, i, b):
        return remote(
            kv.at[b, c], kv.at[b, c], g_s.at[plus, i - 1, b], g_r.at[b], up(i) if plus else down(i)
        )

    def h_copy(b, half):
        return remote(kv.at[b, half], kv.at[b, half], h_s.at[b], h_r.at[b], partner)

    def p_copy(b):
        return remote(acc.at[b, 1 - c], pin.at[b], p_s.at[b], p_r.at[b], partner)

    def r_copy(plus, i, b):
        return remote(
            acc.at[b, c],
            recv.at[plus, i - 1, b],
            r_s.at[b],
            r_r.at[plus, i - 1, b],
            up(i) if plus else down(i),
        )

    def o_copy(kind, to, src):
        return remote(
            oq.at[kind, to], group((att_ref, dq_ref)[kind], src), o_s.at[kind, to], o_r.at[kind, src], at(to, c)
        )

    def f_copy(to, src):
        return remote(okv.at[to], okv_in.at[src], f_s.at[to], f_r.at[src], at(to, c))

    def each_peer(fn):
        @pl.loop(1, PN)
        def _(d):
            fn(lax.rem(me + d, PN))

    def active(b, s):
        return (s > b) | (lax.rem(s, R) == 0)

    barrier = pltpu.get_barrier_semaphore()

    def greet(p):
        for core in range(CORES):
            pl.semaphore_signal(barrier, 1, device_id=at(p, core), device_id_type=MESH)

    pl.semaphore_signal(barrier, 1, device_id=partner, device_id_type=MESH)
    for i in range(1, R + 1):
        pl.semaphore_signal(barrier, 1, device_id=up(i), device_id_type=MESH)
        pl.semaphore_signal(barrier, 1, device_id=down(i), device_id_type=MESH)
    each_peer(greet)

    for l in range(layers):
        narrow[l, 0 : t * G] = k_ref[l].astype(F32).reshape(t * G, width)
        narrow[l, t * G : 2 * t * G] = v_ref[l].astype(F32).reshape(t * G, width)
    for l in range(layers):
        for g in range(G):
            kvp[l * G + g] = narrow[l, pl.ds(g, 2 * t, stride=G), :].astype(BF16)

    pl.semaphore_wait(barrier, 2 * (PN - 1) + 1 + 2 * R)

    def send_kv(p):
        for core in range(CORES):
            kv_copy(p, core, c, me).start()

    each_peer(send_kv)
    kv_copy(me, 1 - c, c, me).start()
    own = [pltpu.make_async_copy(kvp.at[me], kvin.at[c, me], local.at[0])]
    for kind, ref in enumerate((q_ref, g_ref)):
        each_peer(lambda p: q_copy(kind, p, me).start())
        own.append(pltpu.make_async_copy(group(ref, me), qin.at[kind, me], local.at[1 + kind]))
    for copy in own:
        copy.start()

    def land_kv(p):
        for core in range(CORES):
            kv_copy(me, c, core, p).wait_recv()

    own[0].wait()
    kv_copy(me, c, 1 - c, me).wait_recv()
    each_peer(land_kv)
    for h in range(CORES):
        part = kvin[h].astype(F32)
        for s in range(PN):
            for kind in range(2):
                narrow[kind, s * t : (s + 1) * t] = part[s, kind * t : (kind + 1) * t]
        for kind in range(2):
            kv[z, h, kind] = narrow[kind, 0:HK].astype(BF16)

    def relay(b, s):
        for i in range(1, R + 1):

            @pl.when((s + i <= H) & (z + i < NZ))
            def _():
                g_copy(1, i, b).start()

    def relay_down(b, s):
        for i in range(1, R + 1):

            @pl.when((s + i < H) & active(b, s + i))
            def _():
                g_copy(0, i, b).start()

    relay(z, 0)

    @pl.when(z <= H - 2)
    def _():
        relay_down(z, 0)

    for kind, (mine, turned) in enumerate(((qs, qt), (gs, gt))):
        own[1 + kind].wait()
        each_peer(lambda p: q_copy(kind, me, p).wait_recv())
        wide = qin[kind].astype(F32).reshape(rows, width)
        mine[...] = wide.astype(BF16)
        turned[...] = wide.T.astype(BF16)

    def block(b, diagonal=False):
        K = kv[b, :, 0].reshape(BK, width)
        V = kv[b, :, 1].reshape(BK, width)
        scores = dot(K, qt[...])
        if diagonal:
            row = lax.broadcasted_iota(jnp.int32, (1, rows), 1)
            key = lax.broadcasted_iota(jnp.int32, (BK, 1), 0)
            row_token = row // (t * heads) * (2 * t) + c * t + row % (t * heads) // heads
            key_token = key % HK // t * (2 * t) + key // HK * t + key % t
            scores = jnp.where(key_token <= row_token, scores, masked_score)
            top[...] = jnp.max(scores, axis=0, keepdims=True)
        else:
            top[...] = jnp.maximum(top[...], jnp.max(scores, axis=0, keepdims=True))
        sc[b] = scores
        dp[b] = dot(V, gt[...])
        for ref, value in ((kt2, K), (vt2, V)):
            turned = value.astype(F32).T.astype(BF16)
            ref[b, :, 0:BK] = turned
            ref[b, :, BK : 2 * BK] = turned

    block(z, True)

    def lower(s):
        return z - s

    def wrapped(s):
        return lax.rem(z + s, NZ)

    def compute(s):
        b = lower(s)

        @pl.when(b >= 0)
        def _():
            h_copy(b, 1 - c).wait_recv()
            block(b)

        b2 = wrapped(s)

        @pl.when((s < H) & (b2 < z))
        def _():
            h_copy(b2, 1 - c).wait_recv()
            block(b2)

    @pl.loop(1, H + 1)
    def _(s):
        b = lower(s)

        @pl.when(b >= 0)
        def _():
            g_copy(1, 1, b).wait_recv()

            @pl.when(lax.rem(s, R) == 0)
            def _():
                relay(b, s)

            h_copy(b, c).start()

        b2 = wrapped(s)

        @pl.when((s < H) & (b2 <= H - 2) & active(b2, s))
        def _():
            g_copy(0, 1, b2).wait_recv()

            @pl.when(lax.rem(s, R) == 0)
            def _():
                relay_down(b2, s)

            @pl.when(b2 < z)
            def _():
                h_copy(b2, c).start()

        @pl.when(s > 1)
        def _():
            compute(s - 1)

    compute(H)

    highest = top[...]
    top[...] = jnp.zeros_like(top)

    @pl.loop(0, z + 1)
    def _(b):
        e = jnp.exp((sc[b] - highest) * scale)
        sc[b] = e
        top[...] += jnp.sum(e, axis=0, keepdims=True)

    inverse = 1.0 / top[...]
    att_t[...] = jnp.zeros_like(att_t)

    @pl.loop(0, z + 1)
    def _(b):
        prob = sc[b] * inverse
        sc[b] = prob
        high = prob.astype(BF16)
        pb[b, 0:BK] = high
        pb[b, BK : 2 * BK] = (prob - high.astype(F32)).astype(BF16)
        att_t[...] += dot(vt2[b], pb[b])

    rounded = att_t[...].astype(BF16).astype(F32)
    delta = jnp.sum(rounded * gt[...].astype(F32), axis=0, keepdims=True)
    oq[0] = rounded.T.astype(BF16).reshape(PN, t, heads, width)
    each_peer(lambda p: o_copy(0, p, me).start())
    o_own = [
        pltpu.make_async_copy(oq.at[kind, me], group((att_ref, dq_ref)[kind], me), local.at[3 + kind])
        for kind in range(2)
    ]
    o_own[0].start()
    dq_t[...] = jnp.zeros_like(dq_t)

    def back(b):
        ds = sc[b] * (dp[b] - delta)
        high = ds.astype(BF16)
        db[0:BK] = high
        db[BK : 2 * BK] = (ds - high.astype(F32)).astype(BF16)
        both = db[...]
        dq_t[...] += dot(kt2[b], both)
        dk = dot(both, qs[...])
        dv = dot(pb[b], gs[...])
        for kind, value in enumerate((dk, dv)):
            value = value[0:BK] + value[BK : 2 * BK]
            for h in range(CORES):
                acc[b, h, kind] = value[h * HK : (h + 1) * HK]
        p_copy(b).start()

    def stage(s):
        b = lower(s)

        @pl.when(b >= 0)
        def _():
            back(b)

        b2 = wrapped(s)

        @pl.when((s < H) & (b2 < z))
        def _():
            back(b2)

    def children(b, s):
        for i in range(1, R + 1):

            @pl.when((s + i <= H) & (z + i < NZ))
            def _():
                r_copy(0, i, b).wait_recv()
                acc[b, c] += recv[0, i - 1, b]

    def children_up(b, s):
        for i in range(1, R + 1):

            @pl.when((s + i < H) & active(b, s + i))
            def _():
                r_copy(1, i, b).wait_recv()
                acc[b, c] += recv[1, i - 1, b]

    def mine(b):
        p_copy(b).wait_recv()
        acc[b, c] += pin[b]

    def fold(s):
        b = lower(s)

        @pl.when(b >= 0)
        def _():
            mine(b)

            @pl.when(lax.rem(s, R) == 0)
            def _():
                children(b, s)

            for i in range(1, R + 1):

                @pl.when(lax.rem(s - 1, R) + 1 == i)
                def _():
                    r_copy(0, i, b).start()

        b2 = wrapped(s)

        @pl.when((s < H) & (b2 <= H - 2) & active(b2, s))
        def _():
            @pl.when(b2 < z)
            def _():
                mine(b2)

            @pl.when(b2 > z)
            def _():
                acc[b2, c] = jnp.zeros(acc.shape[2:], F32)

            @pl.when(lax.rem(s, R) == 0)
            def _():
                children_up(b2, s)

            for i in range(1, R + 1):

                @pl.when(lax.rem(s - 1, R) + 1 == i)
                def _():
                    r_copy(1, i, b2).start()

    stage(H)

    @pl.loop(0, H - 1)
    def _(j):
        stage(H - 1 - j)
        fold(H - j)

    back(z)
    oq[1] = (dq_t[...] * scale).T.astype(BF16).reshape(PN, t, heads, width)
    each_peer(lambda p: o_copy(1, p, me).start())
    o_own[1].start()
    fold(1)
    mine(z)
    children(z, 0)

    @pl.when(z <= H - 2)
    def _():
        children_up(z, 0)

    total = (acc[z, c, 0] * scale, acc[z, c, 1])
    for kind in range(2):
        for s in range(PN):
            okv_wide = total[kind][s * t : (s + 1) * t]
            narrow[kind * 0 + 0, s * 2 * t + kind * t : s * 2 * t + (kind + 1) * t] = okv_wide
    okv[...] = narrow[0, 0 : PN * 2 * t].reshape(PN, 2 * t, width).astype(BF16)
    each_peer(lambda p: f_copy(p, me).start())
    f_own = pltpu.make_async_copy(okv.at[me], okv_in.at[me], local.at[5])
    f_own.start()

    f_own.wait()
    each_peer(lambda p: f_copy(me, p).wait_recv())
    for l in range(layers):
        narrow[l, 0 : G * 2 * t] = okv_in[l * G : (l + 1) * G].astype(F32).reshape(G * 2 * t, width)
    for l in range(layers):
        for i in range(t):
            gk_ref[l, i] = narrow[l, pl.ds(i, G, stride=2 * t), :].astype(BF16)
            gv_ref[l, i] = narrow[l, pl.ds(t + i, G, stride=2 * t), :].astype(BF16)

    for kind in range(2):
        o_own[kind].wait()

    def finish(p):
        for core in range(CORES):
            kv_copy(p, core, c, me).wait_send()
        for kind in range(2):
            q_copy(kind, p, me).wait_send()
            o_copy(kind, p, me).wait_send()
            o_copy(kind, me, p).wait_recv()
        f_copy(p, me).wait_send()

    each_peer(finish)
    kv_copy(me, 1 - c, c, me).wait_send()
    p_copy(z).wait_send()

    def relayed(b, s):
        for i in range(1, R + 1):

            @pl.when((s + i <= H) & (z + i < NZ))
            def _():
                g_copy(1, i, b).wait_send()

    def relayed_down(b, s):
        for i in range(1, R + 1):

            @pl.when((s + i < H) & active(b, s + i))
            def _():
                g_copy(0, i, b).wait_send()

    relayed(z, 0)

    @pl.when(z <= H - 2)
    def _():
        relayed_down(z, 0)

    @pl.loop(1, H + 1)
    def _(s):
        b = lower(s)

        @pl.when(b >= 0)
        def _():
            h_copy(b, c).wait_send()
            p_copy(b).wait_send()
            r_copy(0, 1, b).wait_send()

            @pl.when(lax.rem(s, R) == 0)
            def _():
                relayed(b, s)

        b2 = wrapped(s)

        @pl.when((s < H) & (b2 <= H - 2) & active(b2, s))
        def _():
            r_copy(1, 1, b2).wait_send()

            @pl.when(b2 < z)
            def _():
                h_copy(b2, c).wait_send()
                p_copy(b2).wait_send()

            @pl.when(lax.rem(s, R) == 0)
            def _():
                relayed_down(b2, s)


def on_device(q, k, v, g):
    layers, t, head_count, width = q.shape
    G = k.shape[2]
    heads = head_count // G
    ctx_n, tp_n = lax.axis_size("ctx"), lax.axis_size("tp")
    nx = tp_n // CORES
    ny = layers * G // nx
    NZ = ctx_n // ny
    PN = nx * ny
    HK = PN * t
    BK = 2 * HK
    rows = PN * t * heads

    vmem = pl.BlockSpec(memory_space=pltpu.VMEM)
    sem = pltpu.SemaphoreType.DMA
    V = pltpu.VMEM
    whole_shape = jax.ShapeDtypeStruct(q.shape, BF16)
    kv_shape = jax.ShapeDtypeStruct(k.shape, BF16)
    deep = max(HK * 2, 2 * t * G)
    return pl.pallas_call(
        partial(kernel, (layers, G, nx, ny, NZ, t, heads, width)),
        out_shape=(whole_shape, whole_shape, kv_shape, kv_shape),
        in_specs=[vmem] * 4,
        out_specs=(vmem,) * 4,
        scratch_shapes=[
            V((2, deep, width), F32),
            V((PN, 2 * t, width), BF16),
            V((CORES, PN, 2 * t, width), BF16),
            V((2, PN, t, heads, width), BF16),
            V((NZ, CORES, 2, HK, width), BF16),
            V((rows, width), BF16),
            V((rows, width), BF16),
            V((width, rows), BF16),
            V((width, rows), BF16),
            V((1, rows), F32),
            V((NZ, BK, rows), F32),
            V((NZ, BK, rows), F32),
            V((NZ, 2 * BK, rows), BF16),
            V((2 * BK, rows), BF16),
            V((NZ, width, 2 * BK), BF16),
            V((NZ, width, 2 * BK), BF16),
            V((width, rows), F32),
            V((width, rows), F32),
            V((NZ, CORES, 2, HK, width), F32),
            V((NZ, 2, HK, width), F32),
            V((2, REACH, NZ, 2, HK, width), F32),
            V((2, PN, t, heads, width), BF16),
            V((PN, 2 * t, width), BF16),
            V((PN, 2 * t, width), BF16),
            sem((CORES, PN)),
            sem((CORES, PN)),
            sem((2, PN)),
            sem((2, PN)),
            sem((2, REACH, NZ)),
            sem((NZ,)),
            sem((NZ,)),
            sem((NZ,)),
            sem((NZ,)),
            sem((NZ,)),
            sem((NZ,)),
            sem((2, REACH, NZ)),
            sem((2, PN)),
            sem((2, PN)),
            sem((PN,)),
            sem((PN,)),
            sem((6,)),
        ],
        compiler_params=pltpu.CompilerParams(collective_id=0, has_side_effects=True),
    )(q, k, v, g)


def solution(mesh):
    spec = P(None, ("ctx", "tp"), None, None)
    return jax.shard_map(
        on_device, mesh=mesh, in_specs=(spec,) * 4, out_specs=(spec,) * 4, check_vma=False
    )
```

time: 312 us -> 92.5 us (0.30)
  the two profiles are of different devices: /device:TPU:193 before, /device:TPU:32 now
where the time goes in v1:
time: 92.5 us; the launch traced here: 92.3 us
  Pallas kernels  88 us (95%)
  local copies, waits for them, and re-layouts  3.65 us (4%)
    pallas_call x1, Pallas kernels, on_device(): pl.pallas_call(partial(kernel, (layers, G, nx, ny, NZ, t, heads, width)),...  88 us
    unnamed x10, local copies, waits for them, and re-layouts  3.65 us

profile of v1, /device:TPU:32, one launch (start us, length us, event | category | flops | bytes accessed | tf_op | source)
XLA Modules:
  0.0 92.3 jit_solution(8970884465395248729)
XLA Ops:
  0.6 88.0 %shard_map.75 = (bf16[2,4,64,128]{3,2,1,0:T(8,128)(2,1)}, bf16[2,4,64,128]{3,2,1,0:T(8,128)(2,1)}, bf16[2,4,8,128]{3,2,1,0:T(8,128)(2,1)}, bf16[2,4,8,128]{3,2,1,0:T(8,128)(2,1)}) custom-call(bf16[2,4,64,128]{3,2,1,0:T(8,128)(2,1)} %q_ref.1, bf16[2,4,8,128]{3,2,1,0:T(8,128)(2,1)} %k_ref.1, bf16[2,4,8,128]{3,2,1,0:T(8,128)(2,1)} %v_ref.1, ...), custom_call_target="tpu_custom_call" | custom-call | tf_op jit(solution)/shard_map/pallas_call | solution.py:542
  88.6 0.0 copy-start
  88.6 1.6 %copy.12 = bf16[2,4,64,128]{3,2,1,0:T(8,128)(2,1)} copy(bf16[2,4,64,128]{3,2,1,0:T(8,128)(2,1)} %get-tuple-element.8) | data formatting | bytes 262144
  90.2 0.0 copy-done
  90.2 0.0 copy-start.2
  90.2 0.7 copy.13
  90.9 0.1 copy-done.2
  90.9 0.0 copy-start.1
  90.9 0.6 copy.14
  91.5 0.1 copy-done.1
  91.7 0.6 copy.15
Async XLA Ops:
  88.6 1.6 %copy-start = (bf16[2,4,64,128]{3,2,1,0:T(8,128)(2,1)S(1)}, bf16[2,4,64,128]{3,2,1,0:T(8,128)(2,1)}, u32[]{:S(2)}) copy-start(bf16[2,4,64,128]{3,2,1,0:T(8,128)(2,1)} %get-tuple-element.9) | copy-start | bytes 393220
  90.2 0.7 copy-start.2
  90.9 0.7 copy-start.1
